TPU v7x, 512 devices: a whole 4x8x8 slice. The times are simulated.
512 devices in a mesh: rows: 64 (over y, z), cols: 8 (over x, core).
Axes of the slice: x: 4, y: 8, z: 8, core: 2. Of those that a mesh axis runs over, the one named last changes fastest.
Arguments:
- residues: int32 [16384, 4096], P('rows', 'cols'), may hold values from 0 to 20, as said below
- dirichlet: float32 [9, 20], replicated, may hold values from 0.02 to 2
- mix_weight: float32 [9], replicated, may hold values from 0.05 to 1
- background: float32 [20], replicated, may hold values from 0.02 to 0.12
Outputs:
- profile: float32 [20, 4096], P(None, 'cols')
- scores: float32 [16384], P('rows')
- weights: float32 [16384], P('rows')
Inputs may be any that keep to these rules, and one draw needn't show every extreme that they name: `residues`: residue codes; 20 stands for a gap.
All inputs are finite; a program needn't handle non-finite values.
Results may differ from a plain program's by a relative error of at most 0.0003.
Values sent between devices are 32-bit elements; how exact they have to be, the bound alone decides.
A program may use at most 64 MiB of HBM per device.

v0:
```python
import functools
import math

import jax
import jax.numpy as jnp
from jax import lax
from jax.experimental import pallas as pl
from jax.experimental.pallas import tpu as pltpu
from jax.sharding import PartitionSpec as P

MESH = pl.DeviceIdType.MESH
ALPHABET = 20
PAIRS = 10
COMPONENTS = 9
ITERS = 3
COUNT_MASS = 64.0
NZ = 8
LANES = 128
HALF = 64
Y_ROWS = 11
S_ROWS = 17

COUNT_Z, MOVE, GATHER, Y0 = 0, 1, 2, 3
Z0 = Y0 + ITERS + 1
C0 = Z0 + ITERS + 1
EXCHANGES = C0 + ITERS + 1
ORDER = (4, 3, 5, 2, 6, 1, 7)

f32 = jnp.float32
bf16 = jnp.bfloat16


def lgamma(x):
    t = x * (x + 3.0)
    z = x + 4.0
    r = 1.0 / z
    r2 = r * r
    series = r * (1.0 / 12.0 + r2 * (-1.0 / 360.0 + r2 * (1.0 / 1260.0 - r2 * (1.0 / 1680.0))))
    return (z - 0.5) * jnp.log(z) - z + (0.9189385332046727 + series) - jnp.log(t * (t + 2.0))


def iota(shape, dim):
    return lax.broadcasted_iota(jnp.int32, shape, dim)


def low(shape):
    return iota(shape, len(shape) - 1) < HALF


def swap(v):
    return pltpu.roll(v, HALF, 1)


def fold(v):
    return v + swap(v)


def over_rows(v):
    return jnp.sum(v, axis=0, keepdims=True)


def over_lanes(v):
    return jnp.sum(v, axis=1, keepdims=True)


def pick(x, rows):
    bits = [(x & (1 << b)) != 0 for b in range(5)]
    a = [jnp.where(bits[0], rows[2 * i + 1], rows[2 * i]) for i in range(10)]
    b = [jnp.where(bits[1], a[2 * i + 1], a[2 * i]) for i in range(5)]
    c = [jnp.where(bits[2], b[1], b[0]), jnp.where(bits[2], b[3], b[2]), jnp.where(bits[2], rows[20], b[4])]
    return jnp.where(bits[4], c[2], jnp.where(bits[3], c[1], c[0]))


def packed(totals):
    first = low((8, LANES))
    rows = []
    for p in range(PAIRS):
        u, v = totals[p], totals[p + PAIRS]
        rows.append(over_rows(jnp.where(first, u, v) + swap(jnp.where(first, v, u))))
    return rows


def kernel(
    dims,
    res_hbm,
    dir_s,
    mix_s,
    bg_s,
    prof_o,
    score_o,
    weight_o,
    res_v,
    stage,
    held,
    cnt_send,
    cbuf,
    ybuf,
    zbuf,
    sbuf,
    pbuf,
    wide,
    pieces,
    val_hi,
    val_mid,
    ones1,
    ones3,
    alpha,
    base,
    strength,
    inv_bg,
    lik,
    counts,
    hen,
    inc,
    raw_s,
    score_s,
    mass_s,
    table,
    in_sem,
    ssem,
    rsem,
):
    ny, nc, seqs, length = dims
    row = lax.axis_index("rows")
    me_c = lax.axis_index("cols")
    me_y, me_z = row // NZ, row % NZ

    def peer(axis, d):
        if axis == "z":
            return (me_y * NZ + (me_z + d) % NZ, me_c)
        if axis == "y":
            return (((me_y + d) % ny) * NZ + me_z, me_c)
        return (row, (me_c + d) % nc)

    size = {"z": NZ, "y": ny, "c": nc}
    mine = {"z": me_z, "y": me_y, "c": me_c}

    barrier = pltpu.get_barrier_semaphore()
    for axis in "yzc":
        for d in range(1, size[axis]):
            pl.semaphore_signal(barrier, inc=1, device_id=peer(axis, d), device_id_type=MESH)
    load = pltpu.make_async_copy(res_hbm, res_v, in_sem)
    load.start()

    def remote(src, dst, number, axis, d):
        return pltpu.make_async_remote_copy(
            src_ref=src,
            dst_ref=dst,
            send_sem=ssem.at[number, d - 1],
            recv_sem=rsem.at[number, d - 1],
            device_id=peer(axis, d),
            device_id_type=MESH,
        )

    def distances(axis):
        n = size[axis]
        return ORDER if n == 8 else tuple(range(1, n))

    def copies(buf, rows, number, axis):
        me = mine[axis]
        own = buf.at[me, pl.ds(0, rows)]
        return [remote(own, own, number, axis, d) for d in distances(axis)]

    def begin(made):
        for copy in made:
            copy.start()

    def arrive(made):
        for copy in made:
            copy.wait_recv()

    def leave(made):
        for copy in made:
            copy.wait_send()

    def total_of(buf, axis):
        s = buf[0]
        for i in range(1, size[axis]):
            s = s + buf[i]
        return s

    row16 = iota((16, LANES), 0)
    low16 = low((16, LANES))
    load.wait()

    for zd in range(NZ):
        block = pl.ds((zd // 2) * LANES, LANES)
        a, b = res_v[0:LANES, block], res_v[LANES : 2 * LANES, block]
        first = low((LANES, LANES))
        if zd % 2 == 0:
            stage[zd] = jnp.where(first, a, swap(b))
        else:
            stage[zd] = jnp.where(first, swap(a), b)

    def count_one(zd, carry):
        def tile(t, totals):
            for u in range(4):
                at = pl.multiple_of(t * 32 + u * 8, 8)
                x = stage[zd, pl.ds(at, 8), :]
                totals = tuple(totals[a] + jnp.where(x == a, 1.0, 0.0) for a in range(ALPHABET))
            return totals

        totals = lax.fori_loop(0, 4, tile, tuple(jnp.zeros((8, LANES), f32) for _ in range(ALPHABET)))
        for p, line in enumerate(packed(totals)):
            cnt_send[zd, p : p + 1, :] = line
        return carry

    lax.fori_loop(0, NZ, count_one, 0)
    cbuf[me_z] = cnt_send[me_z]
    held[me_z] = stage[me_z]

    pl.semaphore_wait(barrier, ny + NZ + nc - 3)

    sent_counts = []
    for d in distances("z"):
        other = (me_z + d) % NZ
        sent_counts.append(
            remote(cnt_send.at[other, pl.ds(0, PAIRS)], cbuf.at[me_z, pl.ds(0, PAIRS)], COUNT_Z, "z", d)
        )
    moved = [remote(stage.at[(me_z + d) % NZ], held.at[me_z], MOVE, "z", d) for d in distances("z")]
    begin(sent_counts)
    begin(moved)

    shape1 = (16, NZ * LANES)
    hit = (iota(shape1, 0) // 2 == iota(shape1, 1) // LANES) & (
        iota(shape1, 0) % 2 == (iota(shape1, 1) % LANES) // HALF
    )
    spread = jnp.where(hit, 1.0, 0.0).astype(bf16)
    ones1[...] = spread
    for i in range(3):
        ones3[16 * i : 16 * i + 16, :] = spread
    low1 = low((1, LANES))
    for k in range(COMPONENTS):
        alpha[k] = jnp.ones((16, LANES), f32)
        for p in range(PAIRS):
            alpha[k, p : p + 1, :] = jnp.where(low1, dir_s[k, p], dir_s[k, p + PAIRS])
    inv_bg[...] = jnp.ones((16, LANES), f32)
    for p in range(PAIRS):
        inv_bg[p : p + 1, :] = jnp.where(low1, bg_s[p], bg_s[p + PAIRS])
    bg = inv_bg[...]
    inv_bg[...] = jnp.where(row16 < PAIRS, over_rows(fold(jnp.where(row16 < PAIRS, bg, 0.0))) / bg, 1.0)
    strength[...] = jnp.ones((16, LANES), f32)
    base[...] = jnp.zeros((16, LANES), f32)
    lik[...] = jnp.ones((16, LANES), f32)
    for k in range(COMPONENTS):
        al = alpha[k]
        strength[k : k + 1, :] = over_rows(fold(jnp.where(row16 < PAIRS, al, 0.0)))
        base[k : k + 1, :] = over_rows(fold(lgamma(al)))
        lik[k : k + 1, :] = jnp.where(low1, mix_s[k], mix_s[k])
    mix = lik[...]
    log_prior = jnp.log(mix) - jnp.log(over_rows(jnp.where(row16 < COMPONENTS, mix, 0.0)))
    base[...] = log_prior + lgamma(strength[...]) - base[...]

    arrive(sent_counts)
    ybuf[0, me_y] = total_of(cbuf, "z")
    ex = copies(ybuf.at[0], Y_ROWS, Y0, "y")
    begin(ex)
    arrive(ex)
    number = jnp.where(row16 < PAIRS, total_of(ybuf.at[0], "y"), 0.0)
    counts[...] = number
    gap = seqs - over_rows(fold(number))
    present = number > 0.5
    distinct = over_rows(fold(jnp.where(present, 1.0, 0.0))) + jnp.where(gap > 0.5, 1.0, 0.0)
    inverse = jnp.where(present, 1.0 / (distinct * jnp.maximum(number, 1.0)), 0.0)
    gap_inverse = jnp.where(gap > 0.5, 1.0 / (distinct * jnp.maximum(gap, 1.0)), 0.0)

    def set_table(lines, gap_line):
        other = swap(lines)
        table[0:PAIRS, :] = jnp.where(low16, lines, other)[0:PAIRS]
        table[PAIRS:ALPHABET, :] = jnp.where(low16, other, lines)[0:PAIRS]
        table[ALPHABET : ALPHABET + 1, :] = gap_line

    def sums_of_table():
        rows = [jnp.broadcast_to(table[a : a + 1, :], (16, LANES)) for a in range(ALPHABET + 1)]

        def group(g, carry):
            at = pl.multiple_of(g * 16, 16)
            for b in range(NZ):
                v = pick(held[b, pl.ds(at, 16), :], rows)
                hi = v.astype(bf16)
                val_hi[pl.ds(at, 16), b * LANES : (b + 1) * LANES] = hi
                val_mid[pl.ds(at, 16), b * LANES : (b + 1) * LANES] = (v - hi.astype(f32)).astype(bf16)
            return carry

        lax.fori_loop(0, LANES // 16, group, 0)
        nt = (((1,), (1,)), ((), ()))
        e = ones1[...]
        return lax.dot_general(e, val_hi[...], nt, preferred_element_type=f32) + lax.dot_general(
            e, val_mid[...], nt, preferred_element_type=f32
        )

    def sum_over_columns(i, part, extra):
        zbuf[i, me_z, 0:16, :] = part
        zbuf[i, me_z, 16:24, :] = extra
        ex = copies(zbuf.at[i], S_ROWS, Z0 + i, "z")
        begin(ex)
        arrive(ex)
        sbuf[i, me_c] = total_of(zbuf.at[i], "z")
        ex = copies(sbuf.at[i], S_ROWS, C0 + i, "c")
        begin(ex)
        arrive(ex)
        return total_of(sbuf.at[i], "c")

    set_table(inverse, gap_inverse)
    arrive(moved)
    hen[...] = sum_over_columns(0, sums_of_table(), jnp.zeros((8, LANES), f32))[0:16] * (1.0 / length)
    inc[...] = jnp.ones((16, LANES), f32)

    def weighted_counts(i):
        def group(g, totals):
            for b in range(NZ):
                at = pl.multiple_of(g * 8, 8)
                x = held[b, pl.ds(at, 8), :]
                w = wide[pl.ds(at, 8), b * LANES : (b + 1) * LANES]
                totals = tuple(totals[a] + jnp.where(x == a, w, 0.0) for a in range(ALPHABET))
            return totals

        totals = lax.fori_loop(0, LANES // 8, group, tuple(jnp.zeros((8, LANES), f32) for _ in range(ALPHABET)))
        for p, line in enumerate(packed(totals)):
            ybuf[i, me_y, p : p + 1, :] = line

    def mixture(frequency):
        column_total = over_rows(fold(frequency))
        for k in range(COMPONENTS):
            lik[k : k + 1, :] = over_rows(lgamma(frequency + alpha[k]))
        lam = fold(lik[...]) + base[...] - lgamma(strength[...] + column_total)
        lam = jnp.where(row16 < COMPONENTS, lam, -1e30)
        e = jnp.exp(lam - jnp.max(lam, axis=0, keepdims=True))
        shares = e / (over_rows(e) * (column_total + strength[...]))
        smoothed = jnp.zeros((16, LANES), f32)
        for k in range(COMPONENTS):
            smoothed = smoothed + shares[k : k + 1, :] * (frequency + alpha[k])
        return jnp.log(smoothed * inv_bg[...])

    gathered = copies(pbuf, PAIRS, GATHER, "z")

    def iteration(it, carry):
        i = it + 1
        raw = hen[...] * inc[...]
        raw_s[...] = raw
        hi = raw.astype(bf16)
        rest = raw - hi.astype(f32)
        mid = rest.astype(bf16)
        pieces[0:16, :] = hi
        pieces[16:32, :] = mid
        pieces[32:48, :] = (rest - mid.astype(f32)).astype(bf16)
        wide[...] = lax.dot_general(
            pieces[...], ones3[...], (((0,), (0,)), ((), ())), preferred_element_type=f32
        )
        weighted_counts(i)
        ybuf[i, me_y, PAIRS : PAIRS + 1, :] = over_rows(raw)
        ex = copies(ybuf.at[i], Y_ROWS, Y0 + i, "y")
        begin(ex)
        arrive(ex)
        whole = total_of(ybuf.at[i], "y")
        mass = over_lanes(whole[PAIRS : PAIRS + 1, :])
        mass_s[...] = jnp.broadcast_to(mass, (8, LANES))
        frequency = jnp.where(row16 < PAIRS, whole, 0.0) * (COUNT_MASS / mass)
        profile = mixture(frequency)

        @pl.when(it == ITERS - 1)
        def _():
            pbuf[me_z] = profile
            begin(gathered)

        set_table(profile, jnp.zeros((1, LANES), f32))
        share = over_rows(jnp.where(row16 < PAIRS, profile * counts[...], 0.0))
        extra = jnp.where(iota((8, LANES), 0) == 0, share, 0.0)
        done = sum_over_columns(i, sums_of_table(), extra)
        scores = done[0:16] * (1.0 / length)
        center = over_lanes(done[16:17, :]) * (1.0 / (length * seqs))
        score_s[...] = scores
        inc[...] = 1.0 / (1.0 + jnp.exp((center - scores) * math.sqrt(length)))
        return carry

    lax.fori_loop(0, ITERS, iteration, 0)

    weights = raw_s[...] * (seqs / mass_s[0:1, :])
    scores = score_s[...]
    own_w, own_s = weights[0:2], scores[0:2]
    for b in range(1, NZ):
        own_w = jnp.where(me_z == b, weights[2 * b : 2 * b + 2], own_w)
        own_s = jnp.where(me_z == b, scores[2 * b : 2 * b + 2], own_s)
    weight_o[...] = own_w
    score_o[...] = own_s

    arrive(gathered)
    for block in range(NZ // 2):
        even, odd = pbuf[2 * block], pbuf[2 * block + 1]
        at = pl.ds(block * LANES, LANES)
        prof_o[0:PAIRS, at] = jnp.where(low16, even, swap(odd))[0:PAIRS]
        prof_o[PAIRS:ALPHABET, at] = jnp.where(low16, swap(even), odd)[0:PAIRS]

    leave(sent_counts)
    leave(moved)
    leave(gathered)
    for i in range(ITERS + 1):
        leave(copies(ybuf.at[i], Y_ROWS, Y0 + i, "y"))
        leave(copies(zbuf.at[i], S_ROWS, Z0 + i, "z"))
        leave(copies(sbuf.at[i], S_ROWS, C0 + i, "c"))


def solution(mesh):
    rows, cols = mesh.shape["rows"], mesh.shape["cols"]
    ny = rows // NZ

    def body(residues, dirichlet, mix_weight, background):
        high, across = residues.shape
        dims = (ny, cols, high * rows, across * cols)
        tile = pltpu.VMEM((16, LANES), f32)
        profile, scores, weights = pl.pallas_call(
            functools.partial(kernel, dims),
            out_shape=(
                jax.ShapeDtypeStruct((ALPHABET, across), f32),
                jax.ShapeDtypeStruct((2, LANES), f32),
                jax.ShapeDtypeStruct((2, LANES), f32),
            ),
            in_specs=[
                pl.BlockSpec(memory_space=pl.ANY),
                pl.BlockSpec(memory_space=pltpu.SMEM),
                pl.BlockSpec(memory_space=pltpu.SMEM),
                pl.BlockSpec(memory_space=pltpu.SMEM),
            ],
            out_specs=[pl.BlockSpec(memory_space=pltpu.VMEM)] * 3,
            scratch_shapes=[
                pltpu.VMEM((high, across), jnp.int32),
                pltpu.VMEM((NZ, LANES, LANES), jnp.int32),
                pltpu.VMEM((NZ, LANES, LANES), jnp.int32),
                pltpu.VMEM((NZ, 16, LANES), f32),
                pltpu.VMEM((NZ, 16, LANES), f32),
                pltpu.VMEM((ITERS + 1, ny, 16, LANES), f32),
                pltpu.VMEM((ITERS + 1, NZ, 24, LANES), f32),
                pltpu.VMEM((ITERS + 1, cols, 24, LANES), f32),
                pltpu.VMEM((NZ, 16, LANES), f32),
                pltpu.VMEM((LANES, NZ * LANES), f32),
                pltpu.VMEM((48, LANES), bf16),
                pltpu.VMEM((LANES, NZ * LANES), bf16),
                pltpu.VMEM((LANES, NZ * LANES), bf16),
                pltpu.VMEM((16, NZ * LANES), bf16),
                pltpu.VMEM((48, NZ * LANES), bf16),
                pltpu.VMEM((COMPONENTS, 16, LANES), f32),
                tile,
                tile,
                tile,
                tile,
                tile,
                tile,
                tile,
                tile,
                tile,
                pltpu.VMEM((8, LANES), f32),
                pltpu.VMEM((24, LANES), f32),
                pltpu.SemaphoreType.DMA,
                pltpu.SemaphoreType.DMA((EXCHANGES, 7)),
                pltpu.SemaphoreType.DMA((EXCHANGES, 7)),
            ],
            compiler_params=pltpu.CompilerParams(collective_id=0, has_side_effects=True),
        )(residues, dirichlet, mix_weight, background)
        return profile, scores.reshape(-1), weights.reshape(-1)

    in_specs = (P("rows", "cols"), P(), P(), P())
    out_specs = (P(None, "cols"), P("rows"), P("rows"))
    return jax.shard_map(body, mesh=mesh, in_specs=in_specs, out_specs=out_specs, check_vma=False)
```

profile of v0, /device:TPU:1, one launch (start us, length us, event | category | flops | bytes accessed | tf_op | source)
XLA Modules:
  0.0 93.6 jit_solution(11637046364213557015)
XLA Ops:
  0.6 90.3 %shard_map.67 = (f32[20,512]{1,0:T(8,128)}, f32[2,128]{1,0:T(2,128)}, f32[2,128]{1,0:T(2,128)}) custom-call(s32[256,512]{1,0:T(8,128)} %res_hbm.1, f32[9,20]{1,0:T(8,128)} %dir_s.1, f32[9]{0:T(128)} %mix_s.1, f32[20]{0:T(128)} %bg_s.1), custom_call_target="tpu_custom_call" | custom-call | tf_op jit(solution)/shard_map/pallas_call | solution.py:411
  91.0 0.0 copy-start.1
  91.0 1.4 %copy.10 = f32[20,512]{1,0:T(8,128)} copy(f32[20,512]{1,0:T(8,128)} %get-tuple-element.12) | data formatting | bytes 81920
  92.4 0.0 copy-done.1
  92.4 0.0 copy-start
  92.4 0.6 copy.11
  93.0 0.1 copy-done
  93.1 0.6 copy.12
Async XLA Ops:
  91.0 1.4 %copy-start.1 = (f32[2,128]{1,0:T(2,128)S(1)}, f32[2,128]{1,0:T(2,128)}, u32[]{:S(2)}) copy-start(f32[2,128]{1,0:T(2,128)} %get-tuple-element.7) | copy-start | bytes 3076
  92.4 0.7 copy-start
where the time goes:
time: 93.9 us; the launch traced here: 93.6 us
  Pallas kernels  90.3 us (96%)
  local copies, waits for them, and re-layouts  2.67 us (3%)
    pallas_call x1, Pallas kernels, body(): pl.pallas_call(functools.partial(kernel, dims), out_shape=(jax.ShapeDtype...  90.3 us
    unnamed x7, local copies, waits for them, and re-layouts  2.67 us

commit v1 on v0

--- a/solution.py
+++ b/solution.py
@@ -83,16 +83,21 @@
 def kernel(
     dims,
     res_hbm,
+    dir_hbm,
+    mix_hbm,
+    bg_hbm,
+    prof_o,
+    score_o,
+    weight_o,
     dir_s,
     mix_s,
     bg_s,
-    prof_o,
-    score_o,
-    weight_o,
     res_v,
     stage,
     held,
     cnt_send,
+    cnt_lo,
+    cnt_hi,
     cbuf,
     ybuf,
     zbuf,
@@ -117,6 +122,7 @@
     mass_s,
     table,
     in_sem,
+    small_sem,
     ssem,
     rsem,
 ):
@@ -141,6 +147,12 @@
             pl.semaphore_signal(barrier, inc=1, device_id=peer(axis, d), device_id_type=MESH)
     load = pltpu.make_async_copy(res_hbm, res_v, in_sem)
     load.start()
+    small = [
+        pltpu.make_async_copy(src, dst, small_sem.at[n])
+        for n, (src, dst) in enumerate(((dir_hbm, dir_s), (mix_hbm, mix_s), (bg_hbm, bg_s)))
+    ]
+    for copy in small:
+        copy.start()
 
     def remote(src, dst, number, axis, d):
         return pltpu.make_async_remote_copy(
@@ -193,16 +205,25 @@
             stage[zd] = jnp.where(first, swap(a), b)
 
     def count_one(zd, carry):
-        def tile(t, totals):
-            for u in range(4):
-                at = pl.multiple_of(t * 32 + u * 8, 8)
-                x = stage[zd, pl.ds(at, 8), :]
-                totals = tuple(totals[a] + jnp.where(x == a, 1.0, 0.0) for a in range(ALPHABET))
-            return totals
-
-        totals = lax.fori_loop(0, 4, tile, tuple(jnp.zeros((8, LANES), f32) for _ in range(ALPHABET)))
-        for p, line in enumerate(packed(totals)):
-            cnt_send[zd, p : p + 1, :] = line
+        fields = [jnp.zeros((8, LANES), jnp.int32) for _ in range(5)]
+        for t in range(LANES // 8):
+            x = stage[zd, t * 8 : t * 8 + 8, :]
+            unit = jnp.left_shift(jnp.ones((8, LANES), jnp.int32), (x & 3) * 8)
+            which = x >> 2
+            fields = [fields[q] + jnp.where(which == q, unit, 0) for q in range(5)]
+        for q in range(5):
+            v = fields[q]
+            for step in (4, 2, 1):
+                v = v + pltpu.roll(v, step, 0)
+            for r in range(4):
+                p = 4 * q + r
+                line = ((v >> (8 * r)) & 255).astype(f32)
+                if p < PAIRS:
+                    cnt_lo[p : p + 1, :] = line[0:1]
+                else:
+                    cnt_hi[p - PAIRS : p - PAIRS + 1, :] = line[0:1]
+        u, v = cnt_lo[...], cnt_hi[...]
+        cnt_send[zd] = jnp.where(low16, u, v) + swap(jnp.where(low16, v, u))
         return carry
 
     lax.fori_loop(0, NZ, count_one, 0)
@@ -221,15 +242,15 @@
     begin(sent_counts)
     begin(moved)
 
-    shape1 = (16, NZ * LANES)
-    hit = (iota(shape1, 0) // 2 == iota(shape1, 1) // LANES) & (
-        iota(shape1, 0) % 2 == (iota(shape1, 1) % LANES) // HALF
-    )
-    spread = jnp.where(hit, 1.0, 0.0).astype(bf16)
-    ones1[...] = spread
-    for i in range(3):
-        ones3[16 * i : 16 * i + 16, :] = spread
+    for b in range(NZ):
+        half = (iota((16, LANES), 1) >= HALF).astype(jnp.int32)
+        spread = jnp.where(row16 == 2 * b + half, 1.0, 0.0).astype(bf16)
+        ones1[:, b * LANES : (b + 1) * LANES] = spread
+        for n in range(3):
+            ones3[16 * n : 16 * n + 16, b * LANES : (b + 1) * LANES] = spread
     low1 = low((1, LANES))
+    for copy in small:
+        copy.wait()
     for k in range(COMPONENTS):
         alpha[k] = jnp.ones((16, LANES), f32)
         for p in range(PAIRS):
@@ -270,19 +291,35 @@
         table[PAIRS:ALPHABET, :] = jnp.where(low16, other, lines)[0:PAIRS]
         table[ALPHABET : ALPHABET + 1, :] = gap_line
 
-    def sums_of_table():
+    def sums_of_table(arriving=None):
         rows = [jnp.broadcast_to(table[a : a + 1, :], (16, LANES)) for a in range(ALPHABET + 1)]
 
-        def group(g, carry):
-            at = pl.multiple_of(g * 16, 16)
-            for b in range(NZ):
-                v = pick(held[b, pl.ds(at, 16), :], rows)
-                hi = v.astype(bf16)
-                val_hi[pl.ds(at, 16), b * LANES : (b + 1) * LANES] = hi
-                val_mid[pl.ds(at, 16), b * LANES : (b + 1) * LANES] = (v - hi.astype(f32)).astype(bf16)
-            return carry
-
-        lax.fori_loop(0, LANES // 16, group, 0)
+        def look_up(b, at):
+            v = pick(held[b, pl.ds(at, 16), :], rows)
+            hi = v.astype(bf16)
+            columns = pl.ds(b * LANES if isinstance(b, int) else pl.multiple_of(b * LANES, LANES), LANES)
+            val_hi[pl.ds(at, 16), columns] = hi
+            val_mid[pl.ds(at, 16), columns] = (v - hi.astype(f32)).astype(bf16)
+
+        if arriving is None:
+
+            def group(g, carry):
+                for b in range(NZ):
+                    look_up(b, pl.multiple_of(g * 16, 16))
+                return carry
+
+            lax.fori_loop(0, LANES // 16, group, 0)
+        else:
+            for b, copy in arriving:
+                if copy is not None:
+                    copy.wait_recv()
+
+                def group(g, carry):
+                    for u in range(4):
+                        look_up(b, pl.multiple_of(g * 64 + u * 16, 16))
+                    return carry
+
+                lax.fori_loop(0, LANES // 64, group, 0)
         nt = (((1,), (1,)), ((), ()))
         e = ones1[...]
         return lax.dot_general(e, val_hi[...], nt, preferred_element_type=f32) + lax.dot_general(
@@ -302,8 +339,10 @@
         return total_of(sbuf.at[i], "c")
 
     set_table(inverse, gap_inverse)
-    arrive(moved)
-    hen[...] = sum_over_columns(0, sums_of_table(), jnp.zeros((8, LANES), f32))[0:16] * (1.0 / length)
+    arriving = [(me_z, None)]
+    for d, copy in zip(distances("z"), moved):
+        arriving.append(((me_z + NZ - d) % NZ, copy))
+    hen[...] = sum_over_columns(0, sums_of_table(arriving), jnp.zeros((8, LANES), f32))[0:16] * (1.0 / length)
     inc[...] = jnp.ones((16, LANES), f32)
 
     def weighted_counts(i):
@@ -338,6 +377,7 @@
         i = it + 1
         raw = hen[...] * inc[...]
         raw_s[...] = raw
+        part_mass = jnp.broadcast_to(over_lanes(over_rows(raw)), (1, LANES))
         hi = raw.astype(bf16)
         rest = raw - hi.astype(f32)
         mid = rest.astype(bf16)
@@ -348,12 +388,12 @@
             pieces[...], ones3[...], (((0,), (0,)), ((), ())), preferred_element_type=f32
         )
         weighted_counts(i)
-        ybuf[i, me_y, PAIRS : PAIRS + 1, :] = over_rows(raw)
+        ybuf[i, me_y, PAIRS : PAIRS + 1, :] = part_mass
         ex = copies(ybuf.at[i], Y_ROWS, Y0 + i, "y")
         begin(ex)
         arrive(ex)
         whole = total_of(ybuf.at[i], "y")
-        mass = over_lanes(whole[PAIRS : PAIRS + 1, :])
+        mass = whole[PAIRS : PAIRS + 1, :]
         mass_s[...] = jnp.broadcast_to(mass, (8, LANES))
         frequency = jnp.where(row16 < PAIRS, whole, 0.0) * (COUNT_MASS / mass)
         profile = mixture(frequency)
@@ -364,11 +404,11 @@
             begin(gathered)
 
         set_table(profile, jnp.zeros((1, LANES), f32))
-        share = over_rows(jnp.where(row16 < PAIRS, profile * counts[...], 0.0))
+        share = over_lanes(over_rows(jnp.where(row16 < PAIRS, profile * counts[...], 0.0)))
         extra = jnp.where(iota((8, LANES), 0) == 0, share, 0.0)
         done = sum_over_columns(i, sums_of_table(), extra)
         scores = done[0:16] * (1.0 / length)
-        center = over_lanes(done[16:17, :]) * (1.0 / (length * seqs))
+        center = done[16:17, :] * (1.0 / (length * seqs))
         score_s[...] = scores
         inc[...] = 1.0 / (1.0 + jnp.exp((center - scores) * math.sqrt(length)))
         return carry
@@ -417,16 +457,21 @@
             ),
             in_specs=[
                 pl.BlockSpec(memory_space=pl.ANY),
-                pl.BlockSpec(memory_space=pltpu.SMEM),
-                pl.BlockSpec(memory_space=pltpu.SMEM),
-                pl.BlockSpec(memory_space=pltpu.SMEM),
+                pl.BlockSpec(memory_space=pl.ANY),
+                pl.BlockSpec(memory_space=pl.ANY),
+                pl.BlockSpec(memory_space=pl.ANY),
             ],
             out_specs=[pl.BlockSpec(memory_space=pltpu.VMEM)] * 3,
             scratch_shapes=[
+                pltpu.SMEM(dirichlet.shape, f32),
+                pltpu.SMEM(mix_weight.shape, f32),
+                pltpu.SMEM(background.shape, f32),
                 pltpu.VMEM((high, across), jnp.int32),
                 pltpu.VMEM((NZ, LANES, LANES), jnp.int32),
                 pltpu.VMEM((NZ, LANES, LANES), jnp.int32),
                 pltpu.VMEM((NZ, 16, LANES), f32),
+                tile,
+                tile,
                 pltpu.VMEM((NZ, 16, LANES), f32),
                 pltpu.VMEM((ITERS + 1, ny, 16, LANES), f32),
                 pltpu.VMEM((ITERS + 1, NZ, 24, LANES), f32),
@@ -451,6 +496,7 @@
                 pltpu.VMEM((8, LANES), f32),
                 pltpu.VMEM((24, LANES), f32),
                 pltpu.SemaphoreType.DMA,
+                pltpu.SemaphoreType.DMA((3,)),
                 pltpu.SemaphoreType.DMA((EXCHANGES, 7)),
                 pltpu.SemaphoreType.DMA((EXCHANGES, 7)),
             ],

time: 93.9 us -> 91.4 us (0.973)
  Pallas kernels: 90.3 us -> 87.9 us
    pallas_call x1, Pallas kernels: 90.3 us -> 87.9 us  [body(): pl.pallas_call(functools.partial(kernel, dims), out_shape=(jax.ShapeDtype...]
where the time goes in v1:
time: 91.4 us; the launch traced here: 91.2 us
  Pallas kernels  87.9 us (96%)
  local copies, waits for them, and re-layouts  2.67 us (3%)
    pallas_call x1, Pallas kernels, body(): pl.pallas_call(functools.partial(kernel, dims), out_shape=(jax.ShapeDtype...  87.9 us
    unnamed x7, local copies, waits for them, and re-layouts  2.67 us

profile of v1, /device:TPU:1, one launch (start us, length us, event | category | flops | bytes accessed | tf_op | source)
XLA Modules:
  0.0 91.2 jit_solution(14851750853842916416)
XLA Ops:
  0.6 87.9 %shard_map.67 = (f32[20,512]{1,0:T(8,128)}, f32[2,128]{1,0:T(2,128)}, f32[2,128]{1,0:T(2,128)}) custom-call(s32[256,512]{1,0:T(8,128)} %res_hbm.1, f32[9,20]{1,0:T(8,128)} %dir_hbm.1, f32[9]{0:T(128)} %mix_hbm.1, f32[20]{0:T(128)} %bg_hbm.1), custom_call_target="tpu_custom_call" | custom-call | tf_op jit(solution)/shard_map/pallas_call | solution.py:451
  88.5 0.0 copy-start.1
  88.5 1.4 %copy.10 = f32[20,512]{1,0:T(8,128)} copy(f32[20,512]{1,0:T(8,128)} %get-tuple-element.12) | data formatting | bytes 81920
  89.9 0.0 copy-done.1
  89.9 0.0 copy-start
  89.9 0.6 copy.11
  90.5 0.1 copy-done
  90.6 0.6 copy.12
Async XLA Ops:
  88.5 1.4 %copy-start.1 = (f32[2,128]{1,0:T(2,128)S(1)}, f32[2,128]{1,0:T(2,128)}, u32[]{:S(2)}) copy-start(f32[2,128]{1,0:T(2,128)} %get-tuple-element.7) | copy-start | bytes 3076
  89.9 0.7 copy-start

commit v2 on v1

--- a/solution.py
+++ b/solution.py
@@ -18,6 +18,7 @@
 LANES = 128
 HALF = 64
 Y_ROWS = 11
+AT_BG = COMPONENTS * (ALPHABET + 1)
 S_ROWS = 17
 
 COUNT_Z, MOVE, GATHER, Y0 = 0, 1, 2, 3
@@ -83,15 +84,10 @@
 def kernel(
     dims,
     res_hbm,
-    dir_hbm,
-    mix_hbm,
-    bg_hbm,
+    par_hbm,
     prof_o,
-    score_o,
-    weight_o,
-    dir_s,
-    mix_s,
-    bg_s,
+    line_o,
+    par_s,
     res_v,
     stage,
     held,
@@ -147,10 +143,7 @@
             pl.semaphore_signal(barrier, inc=1, device_id=peer(axis, d), device_id_type=MESH)
     load = pltpu.make_async_copy(res_hbm, res_v, in_sem)
     load.start()
-    small = [
-        pltpu.make_async_copy(src, dst, small_sem.at[n])
-        for n, (src, dst) in enumerate(((dir_hbm, dir_s), (mix_hbm, mix_s), (bg_hbm, bg_s)))
-    ]
+    small = [pltpu.make_async_copy(par_hbm, par_s, small_sem.at[0])]
     for copy in small:
         copy.start()
 
@@ -254,10 +247,10 @@
     for k in range(COMPONENTS):
         alpha[k] = jnp.ones((16, LANES), f32)
         for p in range(PAIRS):
-            alpha[k, p : p + 1, :] = jnp.where(low1, dir_s[k, p], dir_s[k, p + PAIRS])
+            alpha[k, p : p + 1, :] = jnp.where(low1, par_s[k * ALPHABET + p], par_s[k * ALPHABET + p + PAIRS])
     inv_bg[...] = jnp.ones((16, LANES), f32)
     for p in range(PAIRS):
-        inv_bg[p : p + 1, :] = jnp.where(low1, bg_s[p], bg_s[p + PAIRS])
+        inv_bg[p : p + 1, :] = jnp.where(low1, par_s[AT_BG + p], par_s[AT_BG + p + PAIRS])
     bg = inv_bg[...]
     inv_bg[...] = jnp.where(row16 < PAIRS, over_rows(fold(jnp.where(row16 < PAIRS, bg, 0.0))) / bg, 1.0)
     strength[...] = jnp.ones((16, LANES), f32)
@@ -267,7 +260,7 @@
         al = alpha[k]
         strength[k : k + 1, :] = over_rows(fold(jnp.where(row16 < PAIRS, al, 0.0)))
         base[k : k + 1, :] = over_rows(fold(lgamma(al)))
-        lik[k : k + 1, :] = jnp.where(low1, mix_s[k], mix_s[k])
+        lik[k : k + 1, :] = jnp.where(low1, par_s[COMPONENTS * ALPHABET + k], par_s[COMPONENTS * ALPHABET + k])
     mix = lik[...]
     log_prior = jnp.log(mix) - jnp.log(over_rows(jnp.where(row16 < COMPONENTS, mix, 0.0)))
     base[...] = log_prior + lgamma(strength[...]) - base[...]
@@ -421,8 +414,8 @@
     for b in range(1, NZ):
         own_w = jnp.where(me_z == b, weights[2 * b : 2 * b + 2], own_w)
         own_s = jnp.where(me_z == b, scores[2 * b : 2 * b + 2], own_s)
-    weight_o[...] = own_w
-    score_o[...] = own_s
+    line_o[0:2, :] = own_s
+    line_o[2:4, :] = own_w
 
     arrive(gathered)
     for block in range(NZ // 2):
@@ -448,24 +441,21 @@
         high, across = residues.shape
         dims = (ny, cols, high * rows, across * cols)
         tile = pltpu.VMEM((16, LANES), f32)
-        profile, scores, weights = pl.pallas_call(
+        small = jnp.concatenate([dirichlet.reshape(-1), mix_weight, background])
+        small = jnp.pad(small, (0, 256 - small.shape[0]))
+        profile, lines = pl.pallas_call(
             functools.partial(kernel, dims),
             out_shape=(
                 jax.ShapeDtypeStruct((ALPHABET, across), f32),
-                jax.ShapeDtypeStruct((2, LANES), f32),
-                jax.ShapeDtypeStruct((2, LANES), f32),
+                jax.ShapeDtypeStruct((4, LANES), f32),
             ),
             in_specs=[
                 pl.BlockSpec(memory_space=pl.ANY),
                 pl.BlockSpec(memory_space=pl.ANY),
-                pl.BlockSpec(memory_space=pl.ANY),
-                pl.BlockSpec(memory_space=pl.ANY),
             ],
-            out_specs=[pl.BlockSpec(memory_space=pltpu.VMEM)] * 3,
+            out_specs=[pl.BlockSpec(memory_space=pltpu.VMEM)] * 2,
             scratch_shapes=[
-                pltpu.SMEM(dirichlet.shape, f32),
-                pltpu.SMEM(mix_weight.shape, f32),
-                pltpu.SMEM(background.shape, f32),
+                pltpu.SMEM((256,), f32),
                 pltpu.VMEM((high, across), jnp.int32),
                 pltpu.VMEM((NZ, LANES, LANES), jnp.int32),
                 pltpu.VMEM((NZ, LANES, LANES), jnp.int32),
@@ -500,9 +490,11 @@
                 pltpu.SemaphoreType.DMA((EXCHANGES, 7)),
                 pltpu.SemaphoreType.DMA((EXCHANGES, 7)),
             ],
-            compiler_params=pltpu.CompilerParams(collective_id=0, has_side_effects=True),
-        )(residues, dirichlet, mix_weight, background)
-        return profile, scores.reshape(-1), weights.reshape(-1)
+            compiler_params=pltpu.CompilerParams(
+                collective_id=0, has_side_effects=True, vmem_limit_bytes=56_500_000
+            ),
+        )(residues, small)
+        return profile, lines[0:2].reshape(-1), lines[2:4].reshape(-1)
 
     in_specs = (P("rows", "cols"), P(), P(), P())
     out_specs = (P(None, "cols"), P("rows"), P("rows"))

time: 91.4 us -> 90.2 us (0.987)
    unnamed x7 -> x5, local copies, waits for them, and re-layouts: 2.67 us -> 0.63 us
    reshape x0 -> x2, local copies, waits for them, and re-layouts: none -> 1.35 us  [the longest x1 0.78 us: body(): small = jnp.concatenate([dirichlet.reshape(-1), mix_weight, background])]
where the time goes in v2:
time: 90.2 us; the launch traced here: 90 us
  Pallas kernels  87.2 us (97%)
  local copies, waits for them, and re-layouts  1.98 us (2%)
    pallas_call x1, Pallas kernels, body(): pl.pallas_call(functools.partial(kernel, dims), out_shape=(jax.ShapeDtype...  87.2 us

profile of v2, /device:TPU:1, one launch (start us, length us, event | category | flops | bytes accessed | tf_op | source)
XLA Modules:
  0.0 90.0 jit_solution(15270999887490658440)
XLA Ops:
  0.6 0.0 copy-start
  0.6 0.0 copy-start.1
  0.7 0.8 reshape.15
  1.4 0.0 copy-done
  1.4 0.0 copy-done.1
  1.5 0.1 select_maximum_fusion.par_hbm
  1.5 87.2 %shard_map.67 = (f32[20,512]{1,0:T(8,128)S(1)}, f32[4,128]{1,0:T(4,128)S(1)}) custom-call(s32[256,512]{1,0:T(8,128)} %res_hbm.1, f32[256]{0:T(256)S(1)} %select_maximum_fusion.par_hbm), custom_call_target="tpu_custom_call" | custom-call | tf_op jit(solution)/shard_map/pallas_call | solution.py:446
  88.8 0.6 slice_bitcast_fusion
  89.3 0.6 copy.8
Async XLA Ops:
  0.6 0.8 copy-start
  0.6 0.8 copy-start.1

commit v3 on v2

--- a/solution.py
+++ b/solution.py
@@ -319,7 +319,7 @@
             e, val_mid[...], nt, preferred_element_type=f32
         )
 
-    def sum_over_columns(i, part, extra):
+    def sum_over_columns(i, part, extra, meanwhile=None):
         zbuf[i, me_z, 0:16, :] = part
         zbuf[i, me_z, 16:24, :] = extra
         ex = copies(zbuf.at[i], S_ROWS, Z0 + i, "z")
@@ -328,6 +328,8 @@
         sbuf[i, me_c] = total_of(zbuf.at[i], "z")
         ex = copies(sbuf.at[i], S_ROWS, C0 + i, "c")
         begin(ex)
+        if meanwhile is not None:
+            meanwhile()
         arrive(ex)
         return total_of(sbuf.at[i], "c")
 
@@ -365,6 +367,22 @@
         return jnp.log(smoothed * inv_bg[...])
 
     gathered = copies(pbuf, PAIRS, GATHER, "z")
+
+    def finish_profile():
+        arrive(gathered)
+        for block in range(NZ // 2):
+            even, odd = pbuf[2 * block], pbuf[2 * block + 1]
+            at = pl.ds(block * LANES, LANES)
+            prof_o[0:PAIRS, at] = jnp.where(low16, even, swap(odd))[0:PAIRS]
+            prof_o[PAIRS:ALPHABET, at] = jnp.where(low16, swap(even), odd)[0:PAIRS]
+        leave(sent_counts)
+        leave(moved)
+        leave(gathered)
+        for i in range(ITERS + 1):
+            leave(copies(ybuf.at[i], Y_ROWS, Y0 + i, "y"))
+            leave(copies(zbuf.at[i], S_ROWS, Z0 + i, "z"))
+            if i < ITERS:
+                leave(copies(sbuf.at[i], S_ROWS, C0 + i, "c"))
 
     def iteration(it, carry):
         i = it + 1
@@ -399,7 +417,7 @@
         set_table(profile, jnp.zeros((1, LANES), f32))
         share = over_lanes(over_rows(jnp.where(row16 < PAIRS, profile * counts[...], 0.0)))
         extra = jnp.where(iota((8, LANES), 0) == 0, share, 0.0)
-        done = sum_over_columns(i, sums_of_table(), extra)
+        done = sum_over_columns(i, sums_of_table(), extra, lambda: pl.when(it == ITERS - 1)(finish_profile))
         scores = done[0:16] * (1.0 / length)
         center = done[16:17, :] * (1.0 / (length * seqs))
         score_s[...] = scores
@@ -417,20 +435,7 @@
     line_o[0:2, :] = own_s
     line_o[2:4, :] = own_w
 
-    arrive(gathered)
-    for block in range(NZ // 2):
-        even, odd = pbuf[2 * block], pbuf[2 * block + 1]
-        at = pl.ds(block * LANES, LANES)
-        prof_o[0:PAIRS, at] = jnp.where(low16, even, swap(odd))[0:PAIRS]
-        prof_o[PAIRS:ALPHABET, at] = jnp.where(low16, swap(even), odd)[0:PAIRS]
-
-    leave(sent_counts)
-    leave(moved)
-    leave(gathered)
-    for i in range(ITERS + 1):
-        leave(copies(ybuf.at[i], Y_ROWS, Y0 + i, "y"))
-        leave(copies(zbuf.at[i], S_ROWS, Z0 + i, "z"))
-        leave(copies(sbuf.at[i], S_ROWS, C0 + i, "c"))
+    leave(copies(sbuf.at[ITERS], S_ROWS, C0 + ITERS, "c"))
 
 
 def solution(mesh):

time: 90.2 us -> 89.9 us (level)
  no operation moved by 1% of the time
where the time goes in v3:
time: 89.9 us; the launch traced here: 89.7 us
  Pallas kernels  87 us (97%)
  local copies, waits for them, and re-layouts  1.98 us (2%)
    pallas_call x1, Pallas kernels, body(): pl.pallas_call(functools.partial(kernel, dims), out_shape=(jax.ShapeDtype...  87 us

profile of v3, /device:TPU:1, one launch (start us, length us, event | category | flops | bytes accessed | tf_op | source)
XLA Modules:
  0.0 89.7 jit_solution(11640110723482369362)
XLA Ops:
  0.6 0.0 copy-start
  0.6 0.0 copy-start.1
  0.7 0.8 reshape.15
  1.4 0.0 copy-done
  1.4 0.0 copy-done.1
  1.5 0.1 select_maximum_fusion.par_hbm
  1.5 87.0 %shard_map.67 = (f32[20,512]{1,0:T(8,128)S(1)}, f32[4,128]{1,0:T(4,128)S(1)}) custom-call(s32[256,512]{1,0:T(8,128)} %res_hbm.1, f32[256]{0:T(256)S(1)} %select_maximum_fusion.par_hbm), custom_call_target="tpu_custom_call" | custom-call | tf_op jit(solution)/shard_map/pallas_call | solution.py:451
  88.5 0.6 slice_bitcast_fusion
  89.1 0.6 copy.8
Async XLA Ops:
  0.6 0.8 copy-start
  0.6 0.8 copy-start.1

commit v4 on v3

--- a/solution.py
+++ b/solution.py
@@ -65,7 +65,7 @@
 
 
 def pick(x, rows):
-    bits = [(x & (1 << b)) != 0 for b in range(5)]
+    bits = [(x & (1 << b)) != 0 for b in range(3)] + [x > 7, x > 15]
     a = [jnp.where(bits[0], rows[2 * i + 1], rows[2 * i]) for i in range(10)]
     b = [jnp.where(bits[1], a[2 * i + 1], a[2 * i]) for i in range(5)]
     c = [jnp.where(bits[2], b[1], b[0]), jnp.where(bits[2], b[3], b[2]), jnp.where(bits[2], rows[20], b[4])]

time: 89.9 us -> 89.8 us (level)
  no operation moved by 1% of the time
where the time goes in v4:
time: 89.8 us; the launch traced here: 89.6 us
  Pallas kernels  86.9 us (97%)
  local copies, waits for them, and re-layouts  1.98 us (2%)
    pallas_call x1, Pallas kernels, body(): pl.pallas_call(functools.partial(kernel, dims), out_shape=(jax.ShapeDtype...  86.9 us

profile of v4, /device:TPU:1, one launch (start us, length us, event | category | flops | bytes accessed | tf_op | source)
XLA Modules:
  0.0 89.6 jit_solution(6869435247271379137)
XLA Ops:
  0.6 0.0 copy-start
  0.6 0.0 copy-start.1
  0.7 0.8 reshape.15
  1.4 0.0 copy-done
  1.4 0.0 copy-done.1
  1.5 0.1 select_maximum_fusion.par_hbm
  1.5 86.9 %shard_map.67 = (f32[20,512]{1,0:T(8,128)S(1)}, f32[4,128]{1,0:T(4,128)S(1)}) custom-call(s32[256,512]{1,0:T(8,128)} %res_hbm.1, f32[256]{0:T(256)S(1)} %select_maximum_fusion.par_hbm), custom_call_target="tpu_custom_call" | custom-call | tf_op jit(solution)/shard_map/pallas_call | solution.py:451
  88.4 0.6 slice_bitcast_fusion
  89.0 0.6 copy.8
Async XLA Ops:
  0.6 0.8 copy-start
  0.6 0.8 copy-start.1
